TPU v7x, 128 devices: a whole 4x4x4 slice. The times are simulated.
128 devices in a mesh: row: 16 (over z_lo, x, core), col: 8 (over z_hi, y).
Axes of the slice: x: 4, y: 4, z: 4 (z_hi: 2, z_lo: 2; z = z_hi * 2 + z_lo), core: 2. Of those that a mesh axis runs over, the one named last changes fastest.
Arguments:
- gate_weight: bfloat16 [4096, 14336], P('row', 'col'), may hold values from -6 to 6
- up_weight: bfloat16 [4096, 14336], P('row', 'col'), may hold values from -6 to 6
- down_weight: bfloat16 [14336, 4096], P('row', 'col'), may hold values from -6 to 6
- gate_row_bits: int32 [4096], P('row'), may hold values from 0 to 1
- gate_col_bits: int32 [14336], P('col'), may hold values from 0 to 1
- up_row_bits: int32 [4096], P('row'), may hold values from 0 to 1
- up_col_bits: int32 [14336], P('col'), may hold values from 0 to 1
- down_row_bits: int32 [14336], P('row'), may hold values from 0 to 1
- down_col_bits: int32 [4096], P('col'), may hold values from 0 to 1
- block_order: int32 [7], replicated, may hold values from 0 to 6, each once
Outputs:
- gate_out: bfloat16 [4096, 14336], P('row', 'col')
- up_out: bfloat16 [4096, 14336], P('row', 'col')
- down_out: bfloat16 [14336, 4096], P('row', 'col')
Inputs may be any that keep to these rules, and one draw needn't show every extreme that they name: block_order is a permutation of the 7 block numbers.
All inputs are finite; a program needn't handle non-finite values.
Results may differ from a plain program's by a relative error of at most 0.0013.
Values sent between devices are 32-bit elements; how exact they have to be, the bound alone decides.
A program may use at most 64 MiB of HBM per device.

v0:
```python
import jax
import jax.numpy as jnp
from jax import lax
from jax.experimental import pallas as pl
from jax.experimental.pallas import tpu as pltpu
from jax.sharding import PartitionSpec as P

D = 4096
BLK = 128
GROUPS = 16
HBLOCKS = 7
FACTOR = (D * GROUPS * BLK) ** (-0.5)
MESH = pl.DeviceIdType.MESH
LANES = 6
SLOTS = 6
CHUNK = (128, 256)
CORE_AFTER = (1, 3, 1, 3, 1, 3)
VMEM_LIMIT = 55 * 1024 * 1024


def sylvester(order_size):
    rows = lax.broadcasted_iota(jnp.int32, (order_size, order_size), 0)
    both = jnp.bitwise_and(rows, lax.broadcasted_iota(jnp.int32, rows.shape, 1))
    for shift in (4, 2, 1):
        both = jnp.bitwise_xor(both, jnp.right_shift(both, shift))
    return (1 - 2 * jnp.bitwise_and(both, 1)).astype(jnp.float32)


def signs_of(bits):
    return (1 - 2 * bits).astype(jnp.float32)


def split(values):
    high = values.astype(jnp.bfloat16)
    return high, (values - high.astype(jnp.float32)).astype(jnp.bfloat16)


def dot(left, right):
    return jnp.dot(left, right, preferred_element_type=jnp.float32)


def dot_nt(left, right):
    return lax.dot_general(
        left, right, (((1,), (1,)), ((), ())), preferred_element_type=jnp.float32
    )


def kernel(
    order_ref,
    gate_row,
    gate_col,
    up_row,
    up_col,
    down_row,
    down_col,
    gate_hbm,
    up_hbm,
    down_hbm,
    gate_out,
    up_out,
    down_out,
    own,
    got0,
    got1,
    got2,
    got3,
    got4,
    got5,
    got_core,
    sent,
    gate_in,
    up_in,
    down_in,
    plain,
    gate_left,
    up_left,
    down_right,
    in_sem,
    send_sem,
    recv_sem,
    core_send_sem,
    core_recv_sem,
):
    got = (got0, got1, got2, got3, got4, got5)
    row, col = lax.axis_index("row"), lax.axis_index("col")
    core = lax.rem(row, 2)
    x = lax.rem(lax.div(row, 2), 4)
    z_lo = lax.div(row, 8)
    y = lax.rem(col, 4)
    z_hi = lax.div(col, 4)

    def flip(bit):
        return 1 - bit

    def place(z_lo, x, core, z_hi, y):
        return (z_lo * 8 + x * 2 + core, z_hi * 4 + y)

    def one(v):
        return v + 1 - 2 * lax.rem(v, 2)

    partners = (
        (place(z_lo, one(x), core, z_hi, y), place(z_lo, 3 - x, core, z_hi, y)),
        (place(z_lo, x, core, z_hi, one(y)), place(z_lo, x, core, z_hi, 3 - y)),
        (place(flip(z_lo), x, core, z_hi, y), place(flip(z_lo), x, core, flip(z_hi), y)),
    )
    core_partner = place(z_lo, x, flip(core), z_hi, y)

    def as_sign(bit):
        return (1 - 2 * bit).astype(jnp.float32)

    low = (as_sign(lax.rem(x, 2)), as_sign(lax.rem(y, 2)), as_sign(z_lo))
    high = (as_sign(lax.div(x, 2)), as_sign(lax.div(y, 2)), as_sign(z_hi))
    core_sign = as_sign(core)

    def axis_of(group, slot):
        return (group // 2 + slot // 2) % 3

    def partner(group, slot):
        return partners[axis_of(group, slot)][(slot + group) % 2]

    def source(group, slot):
        if slot == 0:
            return own
        if slot % 2 == 1:
            return sent
        return got_core if CORE_AFTER[group] == slot - 1 else got[slot - 1]

    def copy(group, slot, chunk):
        return pltpu.make_async_remote_copy(
            src_ref=source(group, slot).at[group, chunk],
            dst_ref=got[slot].at[group, chunk],
            send_sem=send_sem.at[slot, group, chunk],
            recv_sem=recv_sem.at[slot, group, chunk],
            device_id=partner(group, slot),
            device_id_type=MESH,
        )

    def core_copy(group, chunk):
        return pltpu.make_async_remote_copy(
            src_ref=got[CORE_AFTER[group]].at[group, chunk],
            dst_ref=got_core.at[group, chunk],
            send_sem=core_send_sem.at[group, chunk],
            recv_sem=core_recv_sem.at[group, chunk],
            device_id=core_partner,
            device_id_type=MESH,
        )

    loads = (
        pltpu.make_async_copy(gate_hbm, gate_in, in_sem.at[0]),
        pltpu.make_async_copy(up_hbm, up_in, in_sem.at[1]),
        pltpu.make_async_copy(down_hbm, down_in, in_sem.at[2]),
    )
    for load in loads:
        load.start()

    barrier = pltpu.get_barrier_semaphore()
    for pair in partners:
        for device in pair:
            pl.semaphore_signal(barrier, inc=1, device_id=device, device_id_type=MESH)
    pl.semaphore_signal(barrier, inc=1, device_id=core_partner, device_id_type=MESH)

    hadamard = sylvester(2 * BLK)
    plain[...] = hadamard.astype(jnp.bfloat16)
    gate_left[...] = (hadamard * signs_of(gate_row[...])).astype(jnp.bfloat16)
    up_left[...] = (hadamard * signs_of(up_row[...])).astype(jnp.bfloat16)
    for half in range(2):
        down_right[half] = (
            hadamard * signs_of(down_col[:, half * 256 : (half + 1) * 256])
        ).astype(jnp.bfloat16)

    def pick(block, pieces):
        chosen = pieces(0)
        for other in range(1, HBLOCKS):
            chosen = jnp.where(block == other, pieces(other), chosen)
        return chosen

    def mix_in(weights, left, col_bits, group, chunk):
        block = order_ref[chunk]

        def both(ref, index):
            return jnp.concatenate([ref(index), ref(index + HBLOCKS)], axis=1)

        pair = pick(block, lambda k: both(lambda i: weights[:, i * BLK : (i + 1) * BLK], k))
        bits = pick(block, lambda k: both(lambda i: col_bits[i : i + 1, :], k))
        upper, lower = split(dot(left[...], pair) * signs_of(bits))
        mixed = dot(upper, plain[...]) + dot(lower, plain[...])
        own[group, chunk] = mixed[:BLK]
        own[group + 1, chunk] = mixed[BLK:]

    def mix_down(chunk):
        block = order_ref[chunk]
        weights = pick(block, lambda k: down_in[k * BLK : (k + 1) * BLK, :])
        bits = pick(block, lambda k: down_row[k : k + 1, :])
        first = dot_nt(weights[:, :256], down_right[0])
        second = dot_nt(weights[:, 256:], down_right[1])
        left = (plain[:BLK, :BLK].astype(jnp.float32) * signs_of(bits)).astype(jnp.bfloat16)
        for group, values in ((4, first + second), (5, first - second)):
            upper, lower = split(values)
            own[group, chunk] = dot(left, upper) + dot(left, lower)

    loads[0].wait()
    loads[1].wait()
    loads[2].wait()

    def spread(chunk, carry):
        mix_in(gate_in, gate_left, gate_col, 0, chunk)

        @pl.when(chunk == 0)
        def _():
            pl.semaphore_wait(barrier, 7)

        @pl.when(chunk > 0)
        def _():
            copy(4, 0, chunk - 1).start()
            copy(5, 0, chunk - 1).start()

        mix_in(up_in, up_left, up_col, 2, chunk)
        copy(0, 0, chunk).start()
        copy(1, 0, chunk).start()
        mix_down(chunk)
        copy(2, 0, chunk).start()
        copy(3, 0, chunk).start()
        return carry

    lax.fori_loop(0, HBLOCKS, spread, 0)
    copy(4, 0, HBLOCKS - 1).start()
    copy(5, 0, HBLOCKS - 1).start()

    def first_half(slot):
        def step(chunk, carry):
            for group in range(LANES):
                axis = axis_of(group, slot)
                q = low[axis] if group % 2 == 0 else low[axis] * high[axis]
                if slot > 0:
                    copy(group, slot - 1, chunk).wait_send()
                copy(group, slot, chunk).wait_recv()
                mine = source(group, slot)[group, chunk]
                theirs = q * got[slot][group, chunk]
                got[slot][group, chunk] = mine + theirs
                sent[group, chunk] = mine - theirs
                if group > 0:
                    copy(group - 1, slot + 1, chunk).start()
            copy(LANES - 1, slot + 1, chunk).start()
            return carry

        lax.fori_loop(0, HBLOCKS, step, 0)

    def combined(group, slot, chunk, scale):
        axis = axis_of(group, slot)
        fk = low[axis] * high[axis] * scale
        fr = scale if group % 2 == 0 else high[axis] * scale
        return fr * got[slot][group, chunk] + fk * got[slot - 1][group, chunk]

    def second_half(slot):
        with_core = [group for group in range(LANES) if CORE_AFTER[group] == slot]

        def step(chunk, carry):
            @pl.when(chunk < HBLOCKS)
            def _():
                ready = None
                for group in range(LANES):
                    copy(group, slot - 1, chunk).wait_send()
                    copy(group, slot, chunk).wait_recv()
                    got[slot][group, chunk] = combined(group, slot, chunk, 1.0)
                    if ready is not None:
                        ready.start()
                    if group in with_core:
                        ready = core_copy(group, chunk)
                    else:
                        ready = copy(group, slot + 1, chunk)
                ready.start()

            @pl.when(chunk > 0)
            def _():
                last = chunk - 1
                ready = None
                for group in with_core:
                    core_copy(group, last).wait_recv()
                    got_core[group, last] = (
                        got_core[group, last] + core_sign * got[slot][group, last]
                    )
                    core_copy(group, last).wait_send()
                    if ready is not None:
                        ready.start()
                    ready = copy(group, slot + 1, last)
                ready.start()

            return carry

        lax.fori_loop(0, HBLOCKS + 1, step, 0)

    def finish(slot):
        def step(chunk, carry):
            first = pl.ds(pl.multiple_of(chunk * BLK, BLK), BLK)
            second = pl.ds(pl.multiple_of((chunk + HBLOCKS) * BLK, BLK), BLK)
            for group in range(LANES):
                copy(group, slot - 1, chunk).wait_send()
                copy(group, slot, chunk).wait_recv()
                copy(group, slot, chunk).wait_send()
                values = combined(group, slot, chunk, FACTOR).astype(jnp.bfloat16)
                half = group % 2
                if group < 4:
                    out = gate_out if group < 2 else up_out
                    rows = pl.ds(half * BLK, BLK)
                    out[rows, first] = values[:, :BLK]
                    out[rows, second] = values[:, BLK:]
                else:
                    down_out[first, half * 256 : (half + 1) * 256] = values
            return carry

        lax.fori_loop(0, HBLOCKS, step, 0)

    for pair in range(3):
        first_half(2 * pair)
        if pair < 2:
            second_half(2 * pair + 1)
        else:
            finish(2 * pair + 1)


def flush(gate_mixed, up_mixed, down_mixed, gate_out, up_out, down_out, sem):
    pairs = ((gate_mixed, gate_out), (up_mixed, up_out), (down_mixed, down_out))
    copies = [pltpu.make_async_copy(a, b, sem.at[i]) for i, (a, b) in enumerate(pairs)]
    for c in copies:
        c.start()
    for c in copies:
        c.wait()


def on_device(
    gate_weight,
    up_weight,
    down_weight,
    gate_row_bits,
    gate_col_bits,
    up_row_bits,
    up_col_bits,
    down_row_bits,
    down_col_bits,
    block_order,
):
    wide = pltpu.VMEM((LANES, HBLOCKS) + CHUNK, jnp.float32)
    square = pltpu.VMEM((256, 256), jnp.bfloat16)
    vmem = pl.BlockSpec(memory_space=pltpu.VMEM)
    hbm = pl.BlockSpec(memory_space=pl.ANY)
    weights = (gate_weight, up_weight, down_weight)
    shapes = tuple(jax.ShapeDtypeStruct(w.shape, jnp.bfloat16) for w in weights)
    mixed = pl.pallas_call(
        kernel,
        out_shape=tuple(pltpu.VMEM(w.shape, jnp.bfloat16) for w in weights),
        in_specs=[pl.BlockSpec(memory_space=pltpu.SMEM)] + [vmem] * 6 + [hbm] * 3,
        out_specs=(vmem,) * 3,
        scratch_shapes=[wide] * 9
        + [pltpu.VMEM(w.shape, jnp.bfloat16) for w in weights]
        + [square] * 3
        + [pltpu.VMEM((2, 256, 256), jnp.bfloat16)]
        + [
            pltpu.SemaphoreType.DMA((3,)),
            pltpu.SemaphoreType.DMA((SLOTS, LANES, HBLOCKS)),
            pltpu.SemaphoreType.DMA((SLOTS, LANES, HBLOCKS)),
            pltpu.SemaphoreType.DMA((LANES, HBLOCKS)),
            pltpu.SemaphoreType.DMA((LANES, HBLOCKS)),
        ],
        compiler_params=pltpu.CompilerParams(
            collective_id=0, has_side_effects=True, vmem_limit_bytes=VMEM_LIMIT
        ),
    )(
        block_order,
        gate_row_bits.reshape(1, -1),
        gate_col_bits.reshape(-1, BLK),
        up_row_bits.reshape(1, -1),
        up_col_bits.reshape(-1, BLK),
        down_row_bits.reshape(-1, BLK),
        down_col_bits.reshape(1, -1),
        *weights,
    )
    return pl.pallas_call(
        flush,
        out_shape=shapes,
        in_specs=[vmem] * 3,
        out_specs=(hbm,) * 3,
        scratch_shapes=[pltpu.SemaphoreType.DMA((3,))],
    )(*(pltpu.with_memory_space_constraint(m, pltpu.VMEM) for m in mixed))


def solution(mesh):
    return jax.shard_map(
        on_device,
        mesh=mesh,
        in_specs=(
            P("row", "col"),
            P("row", "col"),
            P("row", "col"),
            P("row"),
            P("col"),
            P("row"),
            P("col"),
            P("row"),
            P("col"),
            P(),
        ),
        out_specs=(P("row", "col"), P("row", "col"), P("row", "col")),
        check_vma=False,
    )
```

profile of v0, /device:TPU:0, one launch (start us, length us, event | category | flops | bytes accessed | tf_op | source)
XLA Modules:
  0.0 135.5 jit_solution(6166253292944048823)
XLA Ops:
  0.6 133.3 %shard_map.121 = (bf16[256,1792]{1,0:T(8,128)(2,1)S(1)}, bf16[256,1792]{1,0:T(8,128)(2,1)S(1)}, bf16[896,512]{1,0:T(8,128)(2,1)S(1)}) custom-call(s32[7]{0:T(128)} %order_ref.1, s32[1,256]{1,0:T(1,128)} %bitcast.10, s32[14,128]{1,0:T(8,128)} %bitcast.6, s32[1,256]{1,0:T(1,128)} %bitcast.11, s32[14,128]{1,0:T(8,128)} %bitcast.7, s32[7,128]{1,0:T(8,128)} %bitcast.8, ...), custom_call_target="tpu_custom_call" | custom-call | tf_op jit(solution)/shard_map/pallas_call | solution.py:348
  133.9 1.6 %shard_map.122 = (bf16[256,1792]{1,0:T(8,128)(2,1)}, bf16[256,1792]{1,0:T(8,128)(2,1)}, bf16[896,512]{1,0:T(8,128)(2,1)}) custom-call(bf16[256,1792]{1,0:T(8,128)(2,1)S(1)} %get-tuple-element.6.gate_mixed, bf16[256,1792]{1,0:T(8,128)(2,1)S(1)} %get-tuple-element.7.up_mixed, bf16[896,512]{1,0:T(8,128)(2,1)S(1)} %get-tuple-element.8.down_mixed), custom_call_target="tpu_custom_call" | custom-call | tf_op jit(solution)/shard_map/pallas_call | solution.py:377
where the time goes:
time: 136 us; the launch traced here: 135 us
  Pallas kernels  135 us (99%)
    pallas_call x1, Pallas kernels, on_device(): pl.pallas_call(kernel, out_shape=tuple((pltpu.VMEM(w.shape, jnp.bfloat16)...  133 us

commit v1 on v0

v1 whole, which is shorter than its diff:
```python
import jax
import jax.numpy as jnp
from jax import lax
from jax.experimental import pallas as pl
from jax.experimental.pallas import tpu as pltpu
from jax.sharding import PartitionSpec as P

D = 4096
BLK = 128
GROUPS = 16
HBLOCKS = 7
FACTOR = (D * GROUPS * BLK) ** (-0.5)
MESH = pl.DeviceIdType.MESH
LANES = 6
SLOTS = 6
CHUNK = (128, 256)
CORE_AFTER = (1, 1, 1, 3, 3, 3)
RIGHT_AFTER = (3, 3, 3, 1, 1, 1)
VMEM_LIMIT = 55 * 1024 * 1024


def sylvester(order_size):
    rows = lax.broadcasted_iota(jnp.int32, (order_size, order_size), 0)
    both = jnp.bitwise_and(rows, lax.broadcasted_iota(jnp.int32, rows.shape, 1))
    for shift in (4, 2, 1):
        both = jnp.bitwise_xor(both, jnp.right_shift(both, shift))
    return (1 - 2 * jnp.bitwise_and(both, 1)).astype(jnp.float32)


def signs_of(bits):
    return (1 - 2 * bits).astype(jnp.float32)


def split(values):
    high = values.astype(jnp.bfloat16)
    return high, (values - high.astype(jnp.float32)).astype(jnp.bfloat16)


def dot(left, right):
    return jnp.dot(left, right, preferred_element_type=jnp.float32)


def kernel(
    gate_row_hbm,
    gate_col_hbm,
    up_row_hbm,
    up_col_hbm,
    down_row_hbm,
    down_col_hbm,
    gate_hbm,
    up_hbm,
    down_hbm,
    order_hbm,
    gate_out,
    up_out,
    down_out,
    order_out,
    own,
    got0,
    got1,
    got2,
    got3,
    got4,
    got5,
    got_core,
    sent,
    gate_in,
    up_in,
    down_in,
    gate_row,
    gate_col,
    up_row,
    up_col,
    down_row,
    down_col,
    plain,
    gate_left,
    up_left,
    in_sem,
    bits_sem,
    send_sem,
    recv_sem,
    core_send_sem,
    core_recv_sem,
):
    got = (got0, got1, got2, got3, got4, got5)
    row, col = lax.axis_index("row"), lax.axis_index("col")
    core = lax.rem(row, 2)
    x = lax.rem(lax.div(row, 2), 4)
    z_lo = lax.div(row, 8)
    y = lax.rem(col, 4)
    z_hi = lax.div(col, 4)

    def flip(bit):
        return 1 - bit

    def place(z_lo, x, core, z_hi, y):
        return (z_lo * 8 + x * 2 + core, z_hi * 4 + y)

    def one(v):
        return v + 1 - 2 * lax.rem(v, 2)

    partners = (
        (place(z_lo, one(x), core, z_hi, y), place(z_lo, 3 - x, core, z_hi, y)),
        (place(z_lo, x, core, z_hi, one(y)), place(z_lo, x, core, z_hi, 3 - y)),
        (place(flip(z_lo), x, core, z_hi, y), place(flip(z_lo), x, core, flip(z_hi), y)),
    )
    core_partner = place(z_lo, x, flip(core), z_hi, y)

    def as_sign(bit):
        return (1 - 2 * bit).astype(jnp.float32)

    low = (as_sign(lax.rem(x, 2)), as_sign(lax.rem(y, 2)), as_sign(z_lo))
    high = (as_sign(lax.div(x, 2)), as_sign(lax.div(y, 2)), as_sign(z_hi))
    core_sign = as_sign(core)

    def axis_of(group, slot):
        return (group // 2 + slot // 2) % 3

    def partner(group, slot):
        return partners[axis_of(group, slot)][(slot + group) % 2]

    def spare(slot):
        return got[slot - 2] if slot else sent

    def source(group, slot):
        if slot == 0:
            return own
        if slot % 2 == 1:
            return spare(slot - 1)
        return got_core if CORE_AFTER[group] == slot - 1 else got[slot - 1]

    def copy(group, slot, chunk):
        return pltpu.make_async_remote_copy(
            src_ref=source(group, slot).at[group, chunk],
            dst_ref=got[slot].at[group, chunk],
            send_sem=send_sem.at[slot % 2, chunk],
            recv_sem=recv_sem.at[slot, chunk],
            device_id=partner(group, slot),
            device_id_type=MESH,
        )

    def wait_all(slot, chunk):
        every = pltpu.make_async_remote_copy(
            src_ref=got[slot].at[:, chunk],
            dst_ref=got[slot].at[:, chunk],
            send_sem=send_sem.at[slot % 2, chunk],
            recv_sem=recv_sem.at[slot, chunk],
            device_id=core_partner,
            device_id_type=MESH,
        )
        every.wait_recv()
        every.wait_send()

    def core_copy(group, chunk):
        return pltpu.make_async_remote_copy(
            src_ref=got[CORE_AFTER[group]].at[group, chunk],
            dst_ref=got_core.at[group, chunk],
            send_sem=core_send_sem.at[chunk],
            recv_sem=core_recv_sem.at[group // 3, chunk],
            device_id=core_partner,
            device_id_type=MESH,
        )

    def wait_core(slot, chunk):
        half = slot // 2
        part = got_core.at[3 * half : 3 * half + 3, chunk]
        every = pltpu.make_async_remote_copy(
            src_ref=part,
            dst_ref=part,
            send_sem=core_send_sem.at[chunk],
            recv_sem=core_recv_sem.at[half, chunk],
            device_id=core_partner,
            device_id_type=MESH,
        )
        every.wait_recv()
        every.wait_send()

    barrier = pltpu.get_barrier_semaphore()
    for pair in partners:
        for device in pair:
            pl.semaphore_signal(barrier, inc=1, device_id=device, device_id_type=MESH)
    pl.semaphore_signal(barrier, inc=1, device_id=core_partner, device_id_type=MESH)

    def columns(source, target, half, first, blocks):
        lanes = pl.ds((half * HBLOCKS + first) * BLK, blocks * BLK)
        return source.at[:, lanes], target.at[:, lanes]

    def blocks(first, count):
        rows = pl.ds(first * BLK, count * BLK)
        return (
            *(columns(gate_hbm, gate_in, half, first, count) for half in range(2)),
            *(columns(up_hbm, up_in, half, first, count) for half in range(2)),
            (down_hbm.at[rows], down_in.at[rows]),
        )

    bit_loads = [
        pltpu.make_async_copy(source, target, bits_sem.at[i])
        for i, (source, target) in enumerate(
            (
                (gate_row_hbm, gate_row),
                (gate_col_hbm, gate_col),
                (up_row_hbm, up_row),
                (up_col_hbm, up_col),
                (down_row_hbm, down_row),
                (down_col_hbm, down_col),
                (order_hbm, order_out),
            )
        )
    ]
    loads = [
        [
            pltpu.make_async_copy(source, target, in_sem.at[part, i])
            for i, (source, target) in enumerate(pairs)
        ]
        for part, pairs in enumerate((blocks(0, 1), blocks(1, HBLOCKS - 1)))
    ]
    for load in bit_loads + loads[0] + loads[1]:
        load.start()

    hadamard = sylvester(2 * BLK)
    plain[...] = hadamard.astype(jnp.bfloat16)
    for load in bit_loads:
        load.wait()
    gate_left[...] = (hadamard * signs_of(gate_row[...])).astype(jnp.bfloat16)
    up_left[...] = (hadamard * signs_of(up_row[...])).astype(jnp.bfloat16)

    def block_of(chunk):
        if isinstance(chunk, int):
            return pl.ds(chunk * BLK, BLK), pl.ds((chunk + HBLOCKS) * BLK, BLK)
        return (
            pl.ds(pl.multiple_of(chunk * BLK, BLK), BLK),
            pl.ds(pl.multiple_of((chunk + HBLOCKS) * BLK, BLK), BLK),
        )

    def mix_in(weights, left, col_bits, group, chunk):
        for half, lanes in enumerate(block_of(chunk)):
            bits = col_bits[pl.ds(chunk + half * HBLOCKS, 1), :]
            mixed = dot(left[...], weights[:, lanes]) * signs_of(bits)
            out = pl.ds(half * BLK, BLK)
            own[group, chunk, :, out] = mixed[:BLK]
            own[group + 1, chunk, :, out] = mixed[BLK:]

    def mix_down(chunk):
        rows = block_of(chunk)[0]
        left = plain[:BLK, :BLK].astype(jnp.float32) * signs_of(down_row[pl.ds(chunk, 1), :])
        mixed = dot(left.astype(jnp.bfloat16), down_in[rows, :]) * signs_of(down_col[...])
        own[4, chunk] = mixed[:, :256] + mixed[:, 256:]
        own[5, chunk] = mixed[:, :256] - mixed[:, 256:]

    def mix_right(values):
        upper, lower = split(values)
        return dot(upper, plain[...]) + dot(lower, plain[...])

    def spread(chunk, carry, waits=False):
        if waits:
            loads[0][0].wait()
            loads[0][1].wait()
        mix_in(gate_in, gate_left, gate_col, 0, chunk)
        if waits:
            loads[0][2].wait()
            loads[0][3].wait()
        mix_in(up_in, up_left, up_col, 2, chunk)
        if waits:
            pl.semaphore_wait(barrier, 7)
        copy(0, 0, chunk).start()
        copy(1, 0, chunk).start()
        if waits:
            loads[0][4].wait()
        mix_down(chunk)
        copy(2, 0, chunk).start()
        copy(3, 0, chunk).start()
        if waits:
            for load in loads[1]:
                load.wait()
        copy(4, 0, chunk).start()
        copy(5, 0, chunk).start()
        return carry

    spread(0, 0, waits=True)
    lax.fori_loop(1, HBLOCKS, spread, 0)

    def first_half(slot):
        def step(chunk, carry):
            wait_all(slot, chunk)
            for group in range(LANES):
                axis = axis_of(group, slot)
                q = low[axis] if group % 2 == 0 else low[axis] * high[axis]
                mine = source(group, slot)[group, chunk]
                theirs = q * got[slot][group, chunk]
                got[slot][group, chunk] = mine + theirs
                spare(slot)[group, chunk] = mine - theirs
                if group > 0:
                    copy(group - 1, slot + 1, chunk).start()
            copy(LANES - 1, slot + 1, chunk).start()
            return carry

        lax.fori_loop(0, HBLOCKS, step, 0)

    def combined(group, slot, chunk, scale):
        axis = axis_of(group, slot)
        fk = low[axis] * high[axis] * scale
        fr = scale if group % 2 == 0 else high[axis] * scale
        return fr * got[slot][group, chunk] + fk * got[slot - 1][group, chunk]

    def second_half(slot):
        with_core = [group for group in range(LANES) if CORE_AFTER[group] == slot]
        others = [group for group in range(LANES) if CORE_AFTER[group] != slot]

        def step(chunk, carry):
            @pl.when(chunk < HBLOCKS)
            def _():
                wait_all(slot, chunk)
                ready = None
                for group in with_core + others:
                    values = combined(group, slot, chunk, 1.0)
                    if RIGHT_AFTER[group] == slot:
                        values = mix_right(values)
                    got[slot][group, chunk] = values
                    if ready is not None:
                        ready.start()
                    if group in with_core:
                        ready = core_copy(group, chunk)
                    else:
                        ready = copy(group, slot + 1, chunk)
                ready.start()

            @pl.when(chunk > 0)
            def _():
                last = chunk - 1
                wait_core(slot, last)
                ready = None
                for group in with_core:
                    got_core[group, last] = (
                        got_core[group, last] + core_sign * got[slot][group, last]
                    )
                    if ready is not None:
                        ready.start()
                    ready = copy(group, slot + 1, last)
                ready.start()

            return carry

        lax.fori_loop(0, HBLOCKS + 1, step, 0)

    def finish(slot):
        def step(chunk, carry):
            wait_all(slot, chunk)
            for group in range(LANES):
                values = combined(group, slot, chunk, FACTOR).astype(jnp.bfloat16)
                out = (gate_out, up_out, down_out)[group // 2]
                part = pl.ds((group % 2) * CHUNK[group // 4], CHUNK[group // 4])
                if group < 4:
                    out[chunk, part, :] = values
                else:
                    out[chunk, :, part] = values
            return carry

        lax.fori_loop(0, HBLOCKS, step, 0)

    for pair in range(3):
        first_half(2 * pair)
        if pair < 2:
            second_half(2 * pair + 1)
        else:
            finish(2 * pair + 1)


def flush(order_ref, gate_mixed, up_mixed, down_mixed, gate_out, up_out, down_out, sem):
    for block in range(HBLOCKS):
        chosen = order_ref[block]
        for index, mixed, out in ((0, gate_mixed, gate_out), (1, up_mixed, up_out)):
            for half in range(2):
                pltpu.make_async_copy(
                    mixed.at[chosen, :, pl.ds(half * BLK, BLK)],
                    out.at[:, pl.ds((half * HBLOCKS + block) * BLK, BLK)],
                    sem.at[index],
                ).start()
        pltpu.make_async_copy(
            down_mixed.at[chosen], down_out.at[pl.ds(block * BLK, BLK)], sem.at[2]
        ).start()
    for index, out in enumerate((gate_out, up_out, down_out)):
        pltpu.make_async_copy(out, out, sem.at[index]).wait()


def on_device(
    gate_weight,
    up_weight,
    down_weight,
    gate_row_bits,
    gate_col_bits,
    up_row_bits,
    up_col_bits,
    down_row_bits,
    down_col_bits,
    block_order,
):
    wide = pltpu.VMEM((LANES, HBLOCKS) + CHUNK, jnp.float32)
    square = pltpu.VMEM((256, 256), jnp.bfloat16)
    hbm = pl.BlockSpec(memory_space=pl.ANY)
    vmem = pl.BlockSpec(memory_space=pltpu.VMEM)
    weights = (gate_weight, up_weight, down_weight)
    bits = (
        gate_row_bits.reshape(1, -1),
        gate_col_bits.reshape(-1, BLK),
        up_row_bits.reshape(1, -1),
        up_col_bits.reshape(-1, BLK),
        down_row_bits.reshape(-1, BLK),
        down_col_bits.reshape(1, -1),
    )
    in_blocks = pltpu.VMEM((HBLOCKS, 256, 256), jnp.bfloat16)
    *mixed, order = pl.pallas_call(
        kernel,
        out_shape=(in_blocks, in_blocks, pltpu.VMEM((HBLOCKS, 128, 512), jnp.bfloat16), pltpu.SMEM((HBLOCKS,), jnp.int32)),
        in_specs=[hbm] * 10,
        out_specs=(vmem,) * 3 + (pl.BlockSpec(memory_space=pltpu.SMEM),),
        scratch_shapes=[wide] * 9
        + [pltpu.VMEM(w.shape, jnp.bfloat16) for w in weights]
        + [pltpu.VMEM(b.shape, jnp.int32) for b in bits]
        + [square] * 3
        + [
            pltpu.SemaphoreType.DMA((2, 5)),
            pltpu.SemaphoreType.DMA((7,)),
            pltpu.SemaphoreType.DMA((2, HBLOCKS)),
            pltpu.SemaphoreType.DMA((SLOTS, HBLOCKS)),
            pltpu.SemaphoreType.DMA((HBLOCKS,)),
            pltpu.SemaphoreType.DMA((2, HBLOCKS)),
        ],
        compiler_params=pltpu.CompilerParams(
            collective_id=0, has_side_effects=True, vmem_limit_bytes=VMEM_LIMIT
        ),
    )(*bits, *weights, block_order)
    return pl.pallas_call(
        flush,
        out_shape=tuple(jax.ShapeDtypeStruct(w.shape, jnp.bfloat16) for w in weights),
        in_specs=[pl.BlockSpec(memory_space=pltpu.SMEM)] + [vmem] * 3,
        out_specs=(hbm,) * 3,
        scratch_shapes=[pltpu.SemaphoreType.DMA((3,))],
    )(pltpu.with_memory_space_constraint(order, pltpu.SMEM), *(pltpu.with_memory_space_constraint(m, pltpu.VMEM) for m in mixed))


def solution(mesh):
    return jax.shard_map(
        on_device,
        mesh=mesh,
        in_specs=(
            P("row", "col"),
            P("row", "col"),
            P("row", "col"),
            P("row"),
            P("col"),
            P("row"),
            P("col"),
            P("row"),
            P("col"),
            P(),
        ),
        out_specs=(P("row", "col"), P("row", "col"), P("row", "col")),
        check_vma=False,
    )
```

time: 136 us -> 129 us (0.949)
  Pallas kernels: 135 us -> 128 us
    pallas_call x2, Pallas kernels: 135 us -> 128 us  [the longest x1 127 us: on_device(): pl.pallas_call(kernel, out_shape=(in_blocks, in_blocks, pltpu.VMEM((HBLOC...]
where the time goes in v1:
time: 129 us
  Pallas kernels  128 us (99%)
    pallas_call x1, Pallas kernels, on_device(): pl.pallas_call(kernel, out_shape=(in_blocks, in_blocks, pltpu.VMEM((HBLOC...  127 us

profile of v1, /device:TPU:0, one launch (start us, length us, event | category | flops | bytes accessed | tf_op | source)
XLA Modules:
  0.0 129.0 jit_solution(6378236864026172736)
XLA Ops:
  0.6 126.8 %shard_map.121 = (bf16[7,256,256]{2,1,0:T(8,128)(2,1)S(1)}, bf16[7,256,256]{2,1,0:T(8,128)(2,1)S(1)}, bf16[7,128,512]{2,1,0:T(8,128)(2,1)S(1)}, s32[7]{0:T(128)S(4)}) custom-call(s32[1,256]{1,0:T(1,128)} %bitcast.10, s32[14,128]{1,0:T(8,128)} %bitcast.6, s32[1,256]{1,0:T(1,128)} %bitcast.11, s32[14,128]{1,0:T(8,128)} %bitcast.7, s32[7,128]{1,0:T(8,128)} %bitcast.8, ...), custom_call_target="tpu_custom_call" | custom-call | tf_op jit(solution)/shard_map/pallas_call | solution.py:412
  127.4 1.5 %shard_map.122 = (bf16[256,1792]{1,0:T(8,128)(2,1)}, bf16[256,1792]{1,0:T(8,128)(2,1)}, bf16[896,512]{1,0:T(8,128)(2,1)}) custom-call(s32[7]{0:T(128)S(4)} %get-tuple-element.7.order_ref, bf16[7,256,256]{2,1,0:T(8,128)(2,1)S(1)} %get-tuple-element.8.gate_mixed, bf16[7,256,256]{2,1,0:T(8,128)(2,1)S(1)} %get-tuple-element.9.up_mixed, ...), custom_call_target="tpu_custom_call" | custom-call | tf_op jit(solution)/shard_map/pallas_call | solution.py:433

commit v2 on v1

--- a/solution.py
+++ b/solution.py
@@ -14,6 +14,7 @@
 LANES = 6
 SLOTS = 6
 CHUNK = (128, 256)
+UNIT = 3
 CORE_AFTER = (1, 1, 1, 3, 3, 3)
 RIGHT_AFTER = (3, 3, 3, 1, 1, 1)
 VMEM_LIMIT = 55 * 1024 * 1024
@@ -64,13 +65,10 @@
     got5,
     got_core,
     sent,
-    gate_in,
-    up_in,
+    in_pair,
     down_in,
-    gate_row,
-    gate_col,
-    up_row,
-    up_col,
+    in_rows,
+    in_cols,
     down_row,
     down_col,
     plain,
@@ -130,51 +128,75 @@
             return spare(slot - 1)
         return got_core if CORE_AFTER[group] == slot - 1 else got[slot - 1]
 
+    def unit_of(chunk):
+        return chunk // UNIT if isinstance(chunk, int) else lax.div(chunk, UNIT)
+
     def copy(group, slot, chunk):
         return pltpu.make_async_remote_copy(
             src_ref=source(group, slot).at[group, chunk],
             dst_ref=got[slot].at[group, chunk],
-            send_sem=send_sem.at[slot % 2, chunk],
-            recv_sem=recv_sem.at[slot, chunk],
+            send_sem=send_sem.at[slot % 2],
+            recv_sem=recv_sem.at[slot, unit_of(chunk)],
             device_id=partner(group, slot),
             device_id_type=MESH,
         )
 
-    def wait_all(slot, chunk):
-        every = pltpu.make_async_remote_copy(
-            src_ref=got[slot].at[:, chunk],
-            dst_ref=got[slot].at[:, chunk],
-            send_sem=send_sem.at[slot % 2, chunk],
-            recv_sem=recv_sem.at[slot, chunk],
+    def await_chunks(slot, chunk, count):
+        part = got[slot].at[:, pl.ds(chunk, count)]
+        pltpu.make_async_remote_copy(
+            src_ref=part,
+            dst_ref=part,
+            send_sem=send_sem.at[slot % 2],
+            recv_sem=recv_sem.at[slot, unit_of(chunk)],
             device_id=core_partner,
             device_id_type=MESH,
-        )
-        every.wait_recv()
-        every.wait_send()
+        ).wait_recv()
+
+    def await_sends(slot):
+        pltpu.make_async_remote_copy(
+            src_ref=got[slot],
+            dst_ref=got[slot],
+            send_sem=send_sem.at[slot % 2],
+            recv_sem=recv_sem.at[slot, 0],
+            device_id=core_partner,
+            device_id_type=MESH,
+        ).wait_send()
+
+    def arrive(slot, chunk):
+        @pl.when((lax.rem(chunk, UNIT) == 0) & (chunk < HBLOCKS - 1))
+        def _():
+            await_chunks(slot, chunk, UNIT)
+
+        @pl.when(chunk == HBLOCKS - 1)
+        def _():
+            await_chunks(slot, chunk, 1)
+
+        if slot > 0:
+
+            @pl.when(chunk == 0)
+            def _():
+                await_sends(slot - 1)
 
     def core_copy(group, chunk):
         return pltpu.make_async_remote_copy(
             src_ref=got[CORE_AFTER[group]].at[group, chunk],
             dst_ref=got_core.at[group, chunk],
-            send_sem=core_send_sem.at[chunk],
-            recv_sem=core_recv_sem.at[group // 3, chunk],
+            send_sem=core_send_sem.at[0],
+            recv_sem=core_recv_sem.at[group // 3, unit_of(chunk)],
             device_id=core_partner,
             device_id_type=MESH,
         )
 
-    def wait_core(slot, chunk):
-        half = slot // 2
-        part = got_core.at[3 * half : 3 * half + 3, chunk]
+    def await_core(slot, part, recv_unit):
         every = pltpu.make_async_remote_copy(
             src_ref=part,
             dst_ref=part,
-            send_sem=core_send_sem.at[chunk],
-            recv_sem=core_recv_sem.at[half, chunk],
+            send_sem=core_send_sem.at[0],
+            recv_sem=core_recv_sem.at[slot // 2, recv_unit],
             device_id=core_partner,
             device_id_type=MESH,
         )
-        every.wait_recv()
-        every.wait_send()
+        return every
 
     barrier = pltpu.get_barrier_semaphore()
     for pair in partners:
@@ -182,67 +204,65 @@
             pl.semaphore_signal(barrier, inc=1, device_id=device, device_id_type=MESH)
     pl.semaphore_signal(barrier, inc=1, device_id=core_partner, device_id_type=MESH)
 
-    def columns(source, target, half, first, blocks):
-        lanes = pl.ds((half * HBLOCKS + first) * BLK, blocks * BLK)
-        return source.at[:, lanes], target.at[:, lanes]
-
-    def blocks(first, count):
+    def columns(source, index, half, first, count):
+        lanes = pl.ds((half * HBLOCKS + first) * BLK, count * BLK)
+        into = pl.ds((first * 2 + half * count) * BLK, count * BLK)
+        return source.at[:, lanes], in_pair.at[index, :, into]
+
+    def load(first, count, sems):
         rows = pl.ds(first * BLK, count * BLK)
-        return (
-            *(columns(gate_hbm, gate_in, half, first, count) for half in range(2)),
-            *(columns(up_hbm, up_in, half, first, count) for half in range(2)),
-            (down_hbm.at[rows], down_in.at[rows]),
+        copies = [
+            pltpu.make_async_copy(*columns(source, index, half, first, count), sems[0])
+            for index, source in enumerate((gate_hbm, up_hbm))
+            for half in range(2)
+        ]
+        copies.append(pltpu.make_async_copy(down_hbm.at[rows], down_in.at[rows], sems[1]))
+        for c in copies:
+            c.start()
+        pair = in_pair.at[:, :, pl.ds(2 * first * BLK, 2 * count * BLK)]
+        return pltpu.make_async_copy(pair, pair, sems[0]), copies[-1]
+
+    bit_loads = []
+    for i, (sources, target) in enumerate(
+        (
+            ((gate_row_hbm, up_row_hbm), in_rows),
+            ((gate_col_hbm, up_col_hbm), in_cols),
+            ((down_row_hbm,), down_row),
+            ((down_col_hbm,), down_col),
+            ((order_hbm,), order_out),
         )
-
-    bit_loads = [
-        pltpu.make_async_copy(source, target, bits_sem.at[i])
-        for i, (source, target) in enumerate(
-            (
-                (gate_row_hbm, gate_row),
-                (gate_col_hbm, gate_col),
-                (up_row_hbm, up_row),
-                (up_col_hbm, up_col),
-                (down_row_hbm, down_row),
-                (down_col_hbm, down_col),
-                (order_hbm, order_out),
-            )
-        )
-    ]
-    loads = [
-        [
-            pltpu.make_async_copy(source, target, in_sem.at[part, i])
-            for i, (source, target) in enumerate(pairs)
-        ]
-        for part, pairs in enumerate((blocks(0, 1), blocks(1, HBLOCKS - 1)))
-    ]
-    for load in bit_loads + loads[0] + loads[1]:
-        load.start()
+    ):
+        for j, operand in enumerate(sources):
+            into = target if len(sources) == 1 else target.at[j]
+            pltpu.make_async_copy(operand, into, bits_sem.at[i]).start()
+        bit_loads.append(pltpu.make_async_copy(target, target, bits_sem.at[i]))
+    loads = [load(0, 1, (in_sem.at[0], in_sem.at[1]))]
+    loads.append(load(1, HBLOCKS - 1, (in_sem.at[2], in_sem.at[3])))
 
     hadamard = sylvester(2 * BLK)
     plain[...] = hadamard.astype(jnp.bfloat16)
-    for load in bit_loads:
-        load.wait()
-    gate_left[...] = (hadamard * signs_of(gate_row[...])).astype(jnp.bfloat16)
-    up_left[...] = (hadamard * signs_of(up_row[...])).astype(jnp.bfloat16)
-
-    def block_of(chunk):
-        if isinstance(chunk, int):
-            return pl.ds(chunk * BLK, BLK), pl.ds((chunk + HBLOCKS) * BLK, BLK)
-        return (
-            pl.ds(pl.multiple_of(chunk * BLK, BLK), BLK),
-            pl.ds(pl.multiple_of((chunk + HBLOCKS) * BLK, BLK), BLK),
-        )
-
-    def mix_in(weights, left, col_bits, group, chunk):
-        for half, lanes in enumerate(block_of(chunk)):
-            bits = col_bits[pl.ds(chunk + half * HBLOCKS, 1), :]
-            mixed = dot(left[...], weights[:, lanes]) * signs_of(bits)
+    for pending in bit_loads:
+        pending.wait()
+    gate_left[...] = (hadamard * signs_of(in_rows[0])).astype(jnp.bfloat16)
+    up_left[...] = (hadamard * signs_of(in_rows[1])).astype(jnp.bfloat16)
+
+    def mix_in(index, left, chunk):
+        for half in range(2):
+            if isinstance(chunk, int):
+                lanes = pl.ds(half * BLK, BLK)
+            else:
+                lanes = pl.ds(
+                    pl.multiple_of((chunk + 1 + half * (HBLOCKS - 1)) * BLK, BLK), BLK
+                )
+            bits = in_cols[index, pl.ds(chunk + half * HBLOCKS, 1), :]
+            mixed = dot(left[...], in_pair[index, :, lanes]) * signs_of(bits)
             out = pl.ds(half * BLK, BLK)
-            own[group, chunk, :, out] = mixed[:BLK]
-            own[group + 1, chunk, :, out] = mixed[BLK:]
+            own[2 * index, chunk, :, out] = mixed[:BLK]
+            own[2 * index + 1, chunk, :, out] = mixed[BLK:]
 
     def mix_down(chunk):
-        rows = block_of(chunk)[0]
+        first = chunk * BLK
+        rows = pl.ds(first if isinstance(chunk, int) else pl.multiple_of(first, BLK), BLK)
         left = plain[:BLK, :BLK].astype(jnp.float32) * signs_of(down_row[pl.ds(chunk, 1), :])
         mixed = dot(left.astype(jnp.bfloat16), down_in[rows, :]) * signs_of(down_col[...])
         own[4, chunk] = mixed[:, :256] + mixed[:, 256:]
@@ -255,24 +275,20 @@
     def spread(chunk, carry, waits=False):
         if waits:
             loads[0][0].wait()
-            loads[0][1].wait()
-        mix_in(gate_in, gate_left, gate_col, 0, chunk)
-        if waits:
-            loads[0][2].wait()
-            loads[0][3].wait()
-        mix_in(up_in, up_left, up_col, 2, chunk)
+        mix_in(0, gate_left, chunk)
+        mix_in(1, up_left, chunk)
         if waits:
             pl.semaphore_wait(barrier, 7)
         copy(0, 0, chunk).start()
         copy(1, 0, chunk).start()
         if waits:
-            loads[0][4].wait()
+            loads[0][1].wait()
         mix_down(chunk)
         copy(2, 0, chunk).start()
         copy(3, 0, chunk).start()
         if waits:
-            for load in loads[1]:
-                load.wait()
+            loads[1][0].wait()
+            loads[1][1].wait()
         copy(4, 0, chunk).start()
         copy(5, 0, chunk).start()
         return carry
@@ -282,7 +298,7 @@
 
     def first_half(slot):
         def step(chunk, carry):
-            wait_all(slot, chunk)
+            arrive(slot, chunk)
             for group in range(LANES):
                 axis = axis_of(group, slot)
                 q = low[axis] if group % 2 == 0 else low[axis] * high[axis]
@@ -307,28 +323,12 @@
         with_core = [group for group in range(LANES) if CORE_AFTER[group] == slot]
         others = [group for group in range(LANES) if CORE_AFTER[group] != slot]
 
-        def step(chunk, carry):
-            @pl.when(chunk < HBLOCKS)
-            def _():
-                wait_all(slot, chunk)
-                ready = None
-                for group in with_core + others:
-                    values = combined(group, slot, chunk, 1.0)
-                    if RIGHT_AFTER[group] == slot:
-                        values = mix_right(values)
-                    got[slot][group, chunk] = values
-                    if ready is not None:
-                        ready.start()
-                    if group in with_core:
-                        ready = core_copy(group, chunk)
-                    else:
-                        ready = copy(group, slot + 1, chunk)
-                ready.start()
-
-            @pl.when(chunk > 0)
-            def _():
-                last = chunk - 1
-                wait_core(slot, last)
+        def settle(first, count):
+            part = got_core.at[pl.ds(with_core[0], 3), pl.ds(first, count)]
+            await_core(slot, part, unit_of(first)).wait_recv()
+
+            def one_chunk(index, carry):
+                last = first + index
                 ready = None
                 for group in with_core:
                     got_core[group, last] = (
@@ -338,14 +338,42 @@
                         ready.start()
                     ready = copy(group, slot + 1, last)
                 ready.start()
+                return carry
+
+            lax.fori_loop(0, count, one_chunk, 0)
+
+        def step(chunk, carry):
+            arrive(slot, chunk)
+            ready = None
+            for group in with_core + others:
+                values = combined(group, slot, chunk, 1.0)
+                if RIGHT_AFTER[group] == slot:
+                    values = mix_right(values)
+                got[slot][group, chunk] = values
+                if ready is not None:
+                    ready.start()
+                if group in with_core:
+                    ready = core_copy(group, chunk)
+                else:
+                    ready = copy(group, slot + 1, chunk)
+            ready.start()
+
+            @pl.when(lax.rem(chunk, UNIT) == UNIT - 1)
+            def _():
+                settle(chunk - (UNIT - 1), UNIT)
+
+            @pl.when(chunk == HBLOCKS - 1)
+            def _():
+                settle(chunk, 1)
 
             return carry
 
-        lax.fori_loop(0, HBLOCKS + 1, step, 0)
+        lax.fori_loop(0, HBLOCKS, step, 0)
+        await_core(slot, got_core.at[pl.ds(with_core[0], 3)], 0).wait_send()
 
     def finish(slot):
         def step(chunk, carry):
-            wait_all(slot, chunk)
+            arrive(slot, chunk)
             for group in range(LANES):
                 values = combined(group, slot, chunk, FACTOR).astype(jnp.bfloat16)
                 out = (gate_out, up_out, down_out)[group // 2]
@@ -357,6 +385,7 @@
             return carry
 
         lax.fori_loop(0, HBLOCKS, step, 0)
+        await_sends(slot)
 
     for pair in range(3):
         first_half(2 * pair)
@@ -415,16 +444,22 @@
         in_specs=[hbm] * 10,
         out_specs=(vmem,) * 3 + (pl.BlockSpec(memory_space=pltpu.SMEM),),
         scratch_shapes=[wide] * 9
-        + [pltpu.VMEM(w.shape, jnp.bfloat16) for w in weights]
-        + [pltpu.VMEM(b.shape, jnp.int32) for b in bits]
+        + [
+            pltpu.VMEM((2,) + gate_weight.shape, jnp.bfloat16),
+            pltpu.VMEM(down_weight.shape, jnp.bfloat16),
+            pltpu.VMEM((2,) + bits[0].shape, jnp.int32),
+            pltpu.VMEM((2,) + bits[1].shape, jnp.int32),
+            pltpu.VMEM(bits[4].shape, jnp.int32),
+            pltpu.VMEM(bits[5].shape, jnp.int32),
+        ]
         + [square] * 3
         + [
-            pltpu.SemaphoreType.DMA((2, 5)),
-            pltpu.SemaphoreType.DMA((7,)),
-            pltpu.SemaphoreType.DMA((2, HBLOCKS)),
-            pltpu.SemaphoreType.DMA((SLOTS, HBLOCKS)),
-            pltpu.SemaphoreType.DMA((HBLOCKS,)),
-            pltpu.SemaphoreType.DMA((2, HBLOCKS)),
+            pltpu.SemaphoreType.DMA((4,)),
+            pltpu.SemaphoreType.DMA((5,)),
+            pltpu.SemaphoreType.DMA((2,)),
+            pltpu.SemaphoreType.DMA((SLOTS, -(-HBLOCKS // UNIT))),
+            pltpu.SemaphoreType.DMA((1,)),
+            pltpu.SemaphoreType.DMA((2, -(-HBLOCKS // UNIT))),
         ],
         compiler_params=pltpu.CompilerParams(
             collective_id=0, has_side_effects=True, vmem_limit_bytes=VMEM_LIMIT

time: 129 us -> 129 us (level)
  no operation moved by 1% of the time
where the time goes in v2:
time: 129 us; the launch traced here: 128 us
  Pallas kernels  128 us (99%)
    pallas_call x1, Pallas kernels, on_device(): pl.pallas_call(kernel, out_shape=(in_blocks, in_blocks, pltpu.VMEM((HBLOC...  126 us

profile of v2, /device:TPU:0, one launch (start us, length us, event | category | flops | bytes accessed | tf_op | source)
XLA Modules:
  0.0 128.5 jit_solution(6879278247243840753)
XLA Ops:
  0.6 126.3 %shard_map.121 = (bf16[7,256,256]{2,1,0:T(8,128)(2,1)S(1)}, bf16[7,256,256]{2,1,0:T(8,128)(2,1)S(1)}, bf16[7,128,512]{2,1,0:T(8,128)(2,1)S(1)}, s32[7]{0:T(128)S(4)}) custom-call(s32[1,256]{1,0:T(1,128)} %bitcast.10, s32[14,128]{1,0:T(8,128)} %bitcast.6, s32[1,256]{1,0:T(1,128)} %bitcast.11, s32[14,128]{1,0:T(8,128)} %bitcast.7, s32[7,128]{1,0:T(8,128)} %bitcast.8, ...), custom_call_target="tpu_custom_call" | custom-call | tf_op jit(solution)/shard_map/pallas_call | solution.py:441
  126.9 1.5 %shard_map.122 = (bf16[256,1792]{1,0:T(8,128)(2,1)}, bf16[256,1792]{1,0:T(8,128)(2,1)}, bf16[896,512]{1,0:T(8,128)(2,1)}) custom-call(s32[7]{0:T(128)S(4)} %get-tuple-element.7.order_ref, bf16[7,256,256]{2,1,0:T(8,128)(2,1)S(1)} %get-tuple-element.8.gate_mixed, bf16[7,256,256]{2,1,0:T(8,128)(2,1)S(1)} %get-tuple-element.9.up_mixed, ...), custom_call_target="tpu_custom_call" | custom-call | tf_op jit(solution)/shard_map/pallas_call | solution.py:468

commit v3 on v2

--- a/solution.py
+++ b/solution.py
@@ -80,6 +80,7 @@
     recv_sem,
     core_send_sem,
     core_recv_sem,
+    ready,
 ):
     got = (got0, got1, got2, got3, got4, got5)
     row, col = lax.axis_index("row"), lax.axis_index("col")
@@ -199,10 +200,15 @@
         return every
 
     barrier = pltpu.get_barrier_semaphore()
-    for pair in partners:
-        for device in pair:
+    links = [(bits[axis], partners[axis][kind]) for axis in range(3) for kind, bits in enumerate(
+        ((lax.rem(x, 2), lax.rem(y, 2), z_lo), (lax.div(x, 2), lax.div(y, 2), z_hi))
+    )]
+    links.append((flip(core), core_partner))
+    for is_higher, device in links:
+
+        @pl.when(is_higher == 0)
+        def _(device=device):
             pl.semaphore_signal(barrier, inc=1, device_id=device, device_id_type=MESH)
-    pl.semaphore_signal(barrier, inc=1, device_id=core_partner, device_id_type=MESH)
 
     def columns(source, index, half, first, count):
         lanes = pl.ds((half * HBLOCKS + first) * BLK, count * BLK)
@@ -241,6 +247,18 @@
 
     hadamard = sylvester(2 * BLK)
     plain[...] = hadamard.astype(jnp.bfloat16)
+    lower_ends = sum(is_higher for is_higher, _ in links)
+
+    @pl.when(lower_ends > 0)
+    def _():
+        pl.semaphore_wait(barrier, lower_ends)
+
+    for index, (is_higher, device) in enumerate(links):
+
+        @pl.when(is_higher == 1)
+        def _(index=index, device=device):
+            pl.semaphore_signal(ready.at[index], inc=1, device_id=device, device_id_type=MESH)
+
     for pending in bit_loads:
         pending.wait()
     gate_left[...] = (hadamard * signs_of(in_rows[0])).astype(jnp.bfloat16)
@@ -272,29 +290,55 @@
         upper, lower = split(values)
         return dot(upper, plain[...]) + dot(lower, plain[...])
 
-    def spread(chunk, carry, waits=False):
-        if waits:
-            loads[0][0].wait()
+    def send_first(chunk, groups=range(LANES)):
+        for group in groups:
+            copy(group, 0, chunk).start()
+
+    def send_when_ready(groups):
+        for group in groups:
+
+            @pl.when(links[group][0] == 0)
+            def _(group=group):
+                pl.semaphore_wait(ready.at[group], 1)
+                copy(group, 0, 0).start()
+
+    def mix(chunk):
         mix_in(0, gate_left, chunk)
         mix_in(1, up_left, chunk)
-        if waits:
-            pl.semaphore_wait(barrier, 7)
-        copy(0, 0, chunk).start()
-        copy(1, 0, chunk).start()
-        if waits:
-            loads[0][1].wait()
         mix_down(chunk)
-        copy(2, 0, chunk).start()
-        copy(3, 0, chunk).start()
-        if waits:
-            loads[1][0].wait()
-            loads[1][1].wait()
-        copy(4, 0, chunk).start()
-        copy(5, 0, chunk).start()
+
+    loads[0][0].wait()
+    loads[0][1].wait()
+    mix(0)
+    for group in range(LANES):
+
+        @pl.when(links[group][0] == 1)
+        def _(group=group):
+            copy(group, 0, 0).start()
+
+    send_when_ready(range(4))
+    loads[1][0].wait()
+    loads[1][1].wait()
+
+    def spread(chunk, carry):
+        mix(chunk)
+        send_first(chunk)
         return carry
 
-    spread(0, 0, waits=True)
-    lax.fori_loop(1, HBLOCKS, spread, 0)
+    def second(chunk, carry):
+        mix(chunk)
+        send_first(chunk, range(4))
+        return carry
+
+    lax.fori_loop(1, 2, second, 0)
+    send_when_ready(range(4, LANES))
+    send_first(1, range(4, LANES))
+
+    @pl.when(core == 1)
+    def _():
+        pl.semaphore_wait(ready.at[LANES], 1)
+
+    lax.fori_loop(2, HBLOCKS, spread, 0)
 
     def first_half(slot):
         def step(chunk, carry):
@@ -460,6 +504,7 @@
             pltpu.SemaphoreType.DMA((SLOTS, -(-HBLOCKS // UNIT))),
             pltpu.SemaphoreType.DMA((1,)),
             pltpu.SemaphoreType.DMA((2, -(-HBLOCKS // UNIT))),
+            pltpu.SemaphoreType.REGULAR((LANES + 1,)),
         ],
         compiler_params=pltpu.CompilerParams(
             collective_id=0, has_side_effects=True, vmem_limit_bytes=VMEM_LIMIT

time: 129 us -> 128 us (level)
  no operation moved by 1% of the time
where the time goes in v3:
time: 128 us; the launch traced here: 127 us
  Pallas kernels  127 us (99%)
    pallas_call x1, Pallas kernels, on_device(): pl.pallas_call(kernel, out_shape=(in_blocks, in_blocks, pltpu.VMEM((HBLOC...  125 us

profile of v3, /device:TPU:0, one launch (start us, length us, event | category | flops | bytes accessed | tf_op | source)
XLA Modules:
  0.0 127.4 jit_solution(6050142933003390528)
XLA Ops:
  0.6 125.3 %shard_map.121 = (bf16[7,256,256]{2,1,0:T(8,128)(2,1)S(1)}, bf16[7,256,256]{2,1,0:T(8,128)(2,1)S(1)}, bf16[7,128,512]{2,1,0:T(8,128)(2,1)S(1)}, s32[7]{0:T(128)S(4)}) custom-call(s32[1,256]{1,0:T(1,128)} %bitcast.10, s32[14,128]{1,0:T(8,128)} %bitcast.6, s32[1,256]{1,0:T(1,128)} %bitcast.11, s32[14,128]{1,0:T(8,128)} %bitcast.7, s32[7,128]{1,0:T(8,128)} %bitcast.8, ...), custom_call_target="tpu_custom_call" | custom-call | tf_op jit(solution)/shard_map/pallas_call | solution.py:485
  125.9 1.5 %shard_map.122 = (bf16[256,1792]{1,0:T(8,128)(2,1)}, bf16[256,1792]{1,0:T(8,128)(2,1)}, bf16[896,512]{1,0:T(8,128)(2,1)}) custom-call(s32[7]{0:T(128)S(4)} %get-tuple-element.7.order_ref, bf16[7,256,256]{2,1,0:T(8,128)(2,1)S(1)} %get-tuple-element.8.gate_mixed, bf16[7,256,256]{2,1,0:T(8,128)(2,1)S(1)} %get-tuple-element.9.up_mixed, ...), custom_call_target="tpu_custom_call" | custom-call | tf_op jit(solution)/shard_map/pallas_call | solution.py:513

commit v4 on v3

--- a/solution.py
+++ b/solution.py
@@ -199,17 +199,6 @@
         )
         return every
 
-    barrier = pltpu.get_barrier_semaphore()
-    links = [(bits[axis], partners[axis][kind]) for axis in range(3) for kind, bits in enumerate(
-        ((lax.rem(x, 2), lax.rem(y, 2), z_lo), (lax.div(x, 2), lax.div(y, 2), z_hi))
-    )]
-    links.append((flip(core), core_partner))
-    for is_higher, device in links:
-
-        @pl.when(is_higher == 0)
-        def _(device=device):
-            pl.semaphore_signal(barrier, inc=1, device_id=device, device_id_type=MESH)
-
     def columns(source, index, half, first, count):
         lanes = pl.ds((half * HBLOCKS + first) * BLK, count * BLK)
         into = pl.ds((first * 2 + half * count) * BLK, count * BLK)
@@ -217,16 +206,16 @@
 
     def load(first, count, sems):
         rows = pl.ds(first * BLK, count * BLK)
-        copies = [
+        copies = [pltpu.make_async_copy(down_hbm.at[rows], down_in.at[rows], sems[1])]
+        copies += [
             pltpu.make_async_copy(*columns(source, index, half, first, count), sems[0])
             for index, source in enumerate((gate_hbm, up_hbm))
             for half in range(2)
         ]
-        copies.append(pltpu.make_async_copy(down_hbm.at[rows], down_in.at[rows], sems[1]))
         for c in copies:
             c.start()
         pair = in_pair.at[:, :, pl.ds(2 * first * BLK, 2 * count * BLK)]
-        return pltpu.make_async_copy(pair, pair, sems[0]), copies[-1]
+        return pltpu.make_async_copy(pair, pair, sems[0]), copies[0]
 
     bit_loads = []
     for i, (sources, target) in enumerate(
@@ -245,6 +234,17 @@
     loads = [load(0, 1, (in_sem.at[0], in_sem.at[1]))]
     loads.append(load(1, HBLOCKS - 1, (in_sem.at[2], in_sem.at[3])))
 
+    barrier = pltpu.get_barrier_semaphore()
+    links = [(bits[axis], partners[axis][kind]) for axis in range(3) for kind, bits in enumerate(
+        ((lax.rem(x, 2), lax.rem(y, 2), z_lo), (lax.div(x, 2), lax.div(y, 2), z_hi))
+    )]
+    links.append((flip(core), core_partner))
+    for is_higher, device in links:
+
+        @pl.when(is_higher == 0)
+        def _(device=device):
+            pl.semaphore_signal(barrier, inc=1, device_id=device, device_id_type=MESH)
+
     hadamard = sylvester(2 * BLK)
     plain[...] = hadamard.astype(jnp.bfloat16)
     lower_ends = sum(is_higher for is_higher, _ in links)
@@ -258,11 +258,6 @@
         @pl.when(is_higher == 1)
         def _(index=index, device=device):
             pl.semaphore_signal(ready.at[index], inc=1, device_id=device, device_id_type=MESH)
-
-    for pending in bit_loads:
-        pending.wait()
-    gate_left[...] = (hadamard * signs_of(in_rows[0])).astype(jnp.bfloat16)
-    up_left[...] = (hadamard * signs_of(in_rows[1])).astype(jnp.bfloat16)
 
     def mix_in(index, left, chunk):
         for half in range(2):
@@ -307,18 +302,30 @@
         mix_in(1, up_left, chunk)
         mix_down(chunk)
 
+    def send_to_lower(groups):
+        for group in groups:
+
+            @pl.when(links[group][0] == 1)
+            def _(group=group):
+                copy(group, 0, 0).start()
+
+    bit_loads[2].wait()
+    bit_loads[3].wait()
+    loads[0][1].wait()
+    mix_down(0)
+    bit_loads[0].wait()
+    bit_loads[1].wait()
+    gate_left[...] = (hadamard * signs_of(in_rows[0])).astype(jnp.bfloat16)
+    up_left[...] = (hadamard * signs_of(in_rows[1])).astype(jnp.bfloat16)
+    send_to_lower((5, 4))
     loads[0][0].wait()
-    loads[0][1].wait()
-    mix(0)
-    for group in range(LANES):
-
-        @pl.when(links[group][0] == 1)
-        def _(group=group):
-            copy(group, 0, 0).start()
-
-    send_when_ready(range(4))
+    mix_in(0, gate_left, 0)
+    mix_in(1, up_left, 0)
+    send_to_lower(range(4))
+    send_when_ready((0, 2, 4, 1, 3))
     loads[1][0].wait()
     loads[1][1].wait()
+    bit_loads[4].wait()
 
     def spread(chunk, carry):
         mix(chunk)
@@ -327,12 +334,12 @@
 
     def second(chunk, carry):
         mix(chunk)
-        send_first(chunk, range(4))
+        send_first(chunk, range(5))
         return carry
 
     lax.fori_loop(1, 2, second, 0)
-    send_when_ready(range(4, LANES))
-    send_first(1, range(4, LANES))
+    send_when_ready((5,))
+    send_first(1, (5,))
 
     @pl.when(core == 1)
     def _():

time: 128 us -> 128 us (level)
  no operation moved by 1% of the time
where the time goes in v4:
time: 128 us; the launch traced here: 127 us
  Pallas kernels  126 us (98%)
    pallas_call x1, Pallas kernels, on_device(): pl.pallas_call(kernel, out_shape=(in_blocks, in_blocks, pltpu.VMEM((HBLOC...  125 us

profile of v4, /device:TPU:0, one launch (start us, length us, event | category | flops | bytes accessed | tf_op | source)
XLA Modules:
  0.0 127.1 jit_solution(6679498867072345687)
XLA Ops:
  0.6 124.9 %shard_map.121 = (bf16[7,256,256]{2,1,0:T(8,128)(2,1)S(1)}, bf16[7,256,256]{2,1,0:T(8,128)(2,1)S(1)}, bf16[7,128,512]{2,1,0:T(8,128)(2,1)S(1)}, s32[7]{0:T(128)S(4)}) custom-call(s32[1,256]{1,0:T(1,128)} %bitcast.10, s32[14,128]{1,0:T(8,128)} %bitcast.6, s32[1,256]{1,0:T(1,128)} %bitcast.11, s32[14,128]{1,0:T(8,128)} %bitcast.7, s32[7,128]{1,0:T(8,128)} %bitcast.8, ...), custom_call_target="tpu_custom_call" | custom-call | tf_op jit(solution)/shard_map/pallas_call | solution.py:492
  125.6 1.5 %shard_map.122 = (bf16[256,1792]{1,0:T(8,128)(2,1)}, bf16[256,1792]{1,0:T(8,128)(2,1)}, bf16[896,512]{1,0:T(8,128)(2,1)}) custom-call(s32[7]{0:T(128)S(4)} %get-tuple-element.7.order_ref, bf16[7,256,256]{2,1,0:T(8,128)(2,1)S(1)} %get-tuple-element.8.gate_mixed, bf16[7,256,256]{2,1,0:T(8,128)(2,1)S(1)} %get-tuple-element.9.up_mixed, ...), custom_call_target="tpu_custom_call" | custom-call | tf_op jit(solution)/shard_map/pallas_call | solution.py:520

commit v5 on v4

--- a/solution.py
+++ b/solution.py
@@ -245,8 +245,6 @@
         def _(device=device):
             pl.semaphore_signal(barrier, inc=1, device_id=device, device_id_type=MESH)
 
-    hadamard = sylvester(2 * BLK)
-    plain[...] = hadamard.astype(jnp.bfloat16)
     lower_ends = sum(is_higher for is_higher, _ in links)
 
     @pl.when(lower_ends > 0)
@@ -259,6 +257,8 @@
         def _(index=index, device=device):
             pl.semaphore_signal(ready.at[index], inc=1, device_id=device, device_id_type=MESH)
 
+    hadamard = sylvester(2 * BLK)
+    plain[...] = hadamard.astype(jnp.bfloat16)
     def mix_in(index, left, chunk):
         for half in range(2):
             if isinstance(chunk, int):

time: 128 us -> 128 us (level)
  no operation moved by 1% of the time
where the time goes in v5:
time: 128 us; the launch traced here: 127 us
  Pallas kernels  126 us (98%)
    pallas_call x1, Pallas kernels, on_device(): pl.pallas_call(kernel, out_shape=(in_blocks, in_blocks, pltpu.VMEM((HBLOC...  125 us

profile of v5, /device:TPU:0, one launch (start us, length us, event | category | flops | bytes accessed | tf_op | source)
XLA Modules:
  0.0 127.1 jit_solution(8283071621081900056)
XLA Ops:
  0.6 124.9 %shard_map.121 = (bf16[7,256,256]{2,1,0:T(8,128)(2,1)S(1)}, bf16[7,256,256]{2,1,0:T(8,128)(2,1)S(1)}, bf16[7,128,512]{2,1,0:T(8,128)(2,1)S(1)}, s32[7]{0:T(128)S(4)}) custom-call(s32[1,256]{1,0:T(1,128)} %bitcast.10, s32[14,128]{1,0:T(8,128)} %bitcast.6, s32[1,256]{1,0:T(1,128)} %bitcast.11, s32[14,128]{1,0:T(8,128)} %bitcast.7, s32[7,128]{1,0:T(8,128)} %bitcast.8, ...), custom_call_target="tpu_custom_call" | custom-call | tf_op jit(solution)/shard_map/pallas_call | solution.py:492
  125.6 1.5 %shard_map.122 = (bf16[256,1792]{1,0:T(8,128)(2,1)}, bf16[256,1792]{1,0:T(8,128)(2,1)}, bf16[896,512]{1,0:T(8,128)(2,1)}) custom-call(s32[7]{0:T(128)S(4)} %get-tuple-element.7.order_ref, bf16[7,256,256]{2,1,0:T(8,128)(2,1)S(1)} %get-tuple-element.8.gate_mixed, bf16[7,256,256]{2,1,0:T(8,128)(2,1)S(1)} %get-tuple-element.9.up_mixed, ...), custom_call_target="tpu_custom_call" | custom-call | tf_op jit(solution)/shard_map/pallas_call | solution.py:520
